TPU v7x, 256 devices: a whole 4x4x8 slice. The times are simulated.
256 devices in a mesh: seq: 2 (over core), chan: 16 (over y, x), batch: 8 (over z).
Axes of the slice: x: 4, y: 4, z: 8, core: 2. Of those that a mesh axis runs over, the one named last changes fastest.
Arguments:
- ssm_input: bfloat16 [16384, 4096], P(('batch', 'seq'), 'chan'), parts along dimension 0, may hold values from -6 to 6
- gate_z: bfloat16 [16384, 4096], P(('batch', 'seq'), 'chan'), parts along dimension 0, may hold values from -6 to 6
- proj_forward: bfloat16 [2, 16384, 128], P(None, ('batch', 'seq')), parts along dimension 1, may hold values from -2 to 2
- proj_backward: bfloat16 [2, 16384, 128], P(None, ('batch', 'seq')), parts along dimension 1, may hold values from -2 to 2
- step_raw: float32 [2, 64, 16384], P(None, 'chan', ('batch', 'seq')), parts along dimension 2, may hold values from -3 to 3
- head_params: float32 [2, 2, 64], P(None, None, 'chan'), may hold values from -4 to 1, as said below
- skip_gain: float32 [64], P('chan'), may hold values from 0.25 to 2
- norm_gain: float32 [4096], P('chan'), may hold values from 0.5 to 1.5
- out_weight: bfloat16 [4096, 2048], P(None, 'chan'), may hold values from -0.09375 to 0.09375
Outputs:
- mixed: bfloat16 [16384, 2048], P(('batch', 'seq'), 'chan'), parts along dimension 0
There are 8 independent parts, one for each index of `batch`. A program takes and returns all parts, laid end to end along the dimension named above; an argument that names none is the same for every part. Nothing has to cross between parts.
Inputs may be any that keep to these rules, and one draw needn't show every extreme that they name: `head_params`: index 0 of the second dimension holds positive decay rates, index 1 time-step biases.
All inputs are finite; a program needn't handle non-finite values.
Results may differ from a plain program's by a relative error of at most 0.0085.
Values may be sent and summed in bfloat16 or wider, within the bound.
A program may use at most 128 MiB of HBM per device.

v0:
```python
import jax
import jax.numpy as jnp
from jax import lax
from jax.sharding import PartitionSpec as P

SPAN = 256
INNER = 4096


def sent_together(arrays, axis, dim, along):
    columns = [a.reshape(*a.shape[:along], -1) for a in arrays]
    both = jnp.concatenate(columns, axis=along)
    whole, at, done = (lax.all_gather(both, axis, axis=dim, tiled=True), 0, [])
    for a, column in zip(arrays, columns):
        slab = whole[..., at : at + column.shape[along]]
        done.append(slab.reshape(*slab.shape[:along], *a.shape[along:]))
        at += column.shape[along]
    return tuple(done)


def copy_for_each(value, axis):
    copies = jnp.broadcast_to(value, (lax.axis_size(axis), *value.shape))
    return lax.all_to_all(copies, axis, split_axis=0, concat_axis=0, tiled=True)


def taken_together(value, axis):
    everything = copy_for_each(value, axis)
    return jnp.sum(everything, axis=0)


def local_scan(blocks_x, b_rows, c_rows, steps_here, decay_rates):
    cumlog = jnp.cumsum(-decay_rates[None, :, None] * steps_here, axis=2)
    scores = jnp.einsum("cqn,csn->cqs", c_rows, b_rows, preferred_element_type=jnp.float32)
    lower_mask = jnp.tril(jnp.ones((SPAN, SPAN), dtype=bool))
    log_gaps = cumlog[:, :, :, None] - cumlog[:, :, None, :]
    decays = jnp.where(lower_mask, jnp.exp(jnp.where(lower_mask, log_gaps, 0.0)), 0.0)
    weights = (scores[:, None] * decays * steps_here[:, :, None, :]).astype(jnp.bfloat16)
    intra_out = jnp.einsum("chts,cshp->cthp", weights, blocks_x, preferred_element_type=jnp.float32)
    end_logs = cumlog[:, :, -1]
    in_weights = jnp.exp(end_logs[:, :, None] - cumlog) * steps_here
    b_weighted = (b_rows[:, None].astype(jnp.float32) * in_weights[..., None]).astype(jnp.bfloat16)
    block_states = jnp.einsum(
        "cshp,chsn->chpn", blocks_x, b_weighted, preferred_element_type=jnp.float32
    )

    def advance(carried, inputs):
        gain_log, block_state = inputs
        return (jnp.exp(gain_log)[:, None, None] * carried + block_state, carried)

    initial = jnp.zeros(block_states.shape[1:], jnp.float32)
    end_state, entering = lax.scan(advance, initial, (end_logs, block_states))
    before = jnp.cumsum(end_logs, axis=0) - end_logs
    whole_decay = jnp.exp(jnp.sum(end_logs, axis=0))
    return ((intra_out, entering, cumlog, before, c_rows), (whole_decay, end_state))


def finish(pieces, carried):
    intra_out, entering, cumlog, before, c_rows = pieces
    states = entering + jnp.exp(before)[:, :, None, None] * carried[None]
    inter = jnp.einsum("ctn,chpn->cthp", c_rows.astype(jnp.float32), states)
    inter = inter * jnp.exp(cumlog).transpose(0, 2, 1)[..., None]
    outputs = intra_out + inter
    return outputs.reshape(outputs.shape[0] * outputs.shape[1], -1)


def body(
    ssm_input,
    gate_z,
    proj_forward,
    proj_backward,
    step_raw,
    head_params,
    skip_gain,
    norm_gain,
    out_weight,
):
    frames, inner_here = ssm_input.shape
    heads_here = step_raw.shape[1]
    width = inner_here // heads_here
    blocks = frames // SPAN
    shape_x = (blocks, SPAN, heads_here, width)
    shape_rows = (blocks, SPAN, proj_forward.shape[2])

    def to_blocks(steps):
        return steps.reshape(heads_here, blocks, SPAN).transpose(1, 0, 2)

    steps_fwd = jax.nn.softplus(step_raw[0] + head_params[0, 1][:, None])
    steps_bwd = jax.nn.softplus(step_raw[1] + head_params[1, 1][:, None])[:, ::-1]
    fwd_parts, fwd_end = local_scan(
        ssm_input.reshape(shape_x),
        proj_forward[0].reshape(shape_rows),
        proj_forward[1].reshape(shape_rows),
        to_blocks(steps_fwd),
        head_params[0, 0],
    )
    bwd_parts, bwd_end = local_scan(
        ssm_input[::-1].reshape(shape_x),
        proj_backward[0][::-1].reshape(shape_rows),
        proj_backward[1][::-1].reshape(shape_rows),
        to_blocks(steps_bwd),
        head_params[1, 0],
    )
    decays_all, states_all = tuple(
        (
            part.astype(jnp.float32)
            for part in sent_together(
                (
                    jnp.stack([fwd_end[0], bwd_end[0]])[None].astype(jnp.bfloat16),
                    jnp.stack([fwd_end[1], bwd_end[1]])[None].astype(jnp.bfloat16),
                ),
                "seq",
                0,
                3,
            )
        )
    )
    own_index = lax.axis_index("seq")
    group_size = lax.axis_size("seq")

    def accumulate(position, carried):
        forward_state, backward_state = carried
        mirror = group_size - 1 - position
        forward_state = jnp.where(
            position < own_index,
            decays_all[position, 0][:, None, None] * forward_state + states_all[position, 0],
            forward_state,
        )
        backward_state = jnp.where(
            mirror > own_index,
            decays_all[mirror, 1][:, None, None] * backward_state + states_all[mirror, 1],
            backward_state,
        )
        return (forward_state, backward_state)

    empty_state = jnp.zeros(fwd_end[1].shape, jnp.float32)
    carry_fwd, carry_bwd = lax.fori_loop(0, group_size, accumulate, (empty_state, empty_state))
    forward_out = finish(fwd_parts, carry_fwd)
    backward_out = finish(bwd_parts, carry_bwd)[::-1]
    skipped = (
        ssm_input.reshape(frames, heads_here, width).astype(jnp.float32) * skip_gain[:, None]
    ).reshape(frames, inner_here)
    gated = (forward_out + backward_out + skipped) * jax.nn.silu(gate_z.astype(jnp.float32))
    squares = taken_together(jnp.sum(gated * gated, axis=1), "chan")
    scale = lax.rsqrt(squares / INNER + 1.0)
    normed = (gated * scale[:, None] * norm_gain).astype(jnp.bfloat16)
    frame_share = lax.all_to_all(normed, "chan", split_axis=0, concat_axis=1, tiled=True)
    projected = jnp.dot(
        frame_share,
        lax.all_gather(out_weight, "chan", axis=1, tiled=True),
        preferred_element_type=jnp.float32,
    ).astype(jnp.bfloat16)
    return lax.all_to_all(projected, "chan", split_axis=1, concat_axis=0, tiled=True)


def solution(mesh):
    in_specs = (
        P(("batch", "seq"), "chan"),
        P(("batch", "seq"), "chan"),
        P(None, ("batch", "seq"), None),
        P(None, ("batch", "seq"), None),
        P(None, "chan", ("batch", "seq")),
        P(None, None, "chan"),
        P("chan"),
        P("chan"),
        P(None, "chan"),
    )
    out_specs = P(("batch", "seq"), "chan")
    return jax.shard_map(body, mesh=mesh, in_specs=in_specs, out_specs=out_specs, check_vma=False)
```

profile of v0, /device:TPU:96, one launch (start us, length us, event | category | flops | bytes accessed | tf_op | source)
XLA Modules:
  0.0 171.4 jit_solution(11320585137728651989)
XLA Ops:
  6.5 0.7 all-gather.2.cloned.1.call-update
  7.3 1.2 copy.167
  8.5 6.3 %rev.17 = bf16[1024,256]{1,0:T(8,128)(2,1)S(1)} reverse(bf16[1024,256]{1,0:T(8,128)(2,1)} %param.15), dimensions={0} | reverse | bytes 1048576 | tf_op jit(solution)/shard_map/rev | solution.py:97
  14.9 0.7 slice.57
  15.6 0.8 negate_bitcast_fusion
  16.4 0.8 compare_select_fusion
  17.2 0.7 rev.15
  18.0 4.8 %reduce-window.14 = f32[4,4,2,128]{3,2,1,0:T(2,128)S(1)} reduce-window(f32[4,4,2,128]{3,2,1,0:T(2,128)S(1)} %reshape.296, f32[]{:T(128)} %constant.83.clone.1), window={size=1x1x1x128 pad=0_0x0_0x0_0x127_0}, to_apply=%region_0.1 | reduce-window | flops 520192 | bytes 32772 | tf_op jit(solution)/shard_map/reduce-window
  23.6 1.1 fusion.56
  24.8 1.2 reshape.298
  26.0 0.6 exponential_multiply_fusion.1
  26.6 1.9 %convolution_bitcast_fusion.3 = f32[4,4,64,128]{3,2,1,0:T(8,128)S(1)} fusion(f32[4,4,256]{2,1,0:T(4,128)S(1)} %get-tuple-element.329, f32[4,256,128]{2,1,0:T(8,128)S(1)} %convert_element_type.76, bf16[4,256,4,64]{1,0,3,2:T(4,128)(2,1)} %reshape.298), kind=kOutput, calls=%fused_computation.48 | convolution fusion | flops 68157440 | bytes 1589248 | tf_op jit(solution)/shard_map/cshp,chsn->chpn/dot_general | solution.py:42
  28.6 0.6 while.44
  29.3 4.8 %reduce-window.16 = f32[4,4,2,128]{3,2,1,0:T(2,128)S(1)} reduce-window(f32[4,4,2,128]{3,2,1,0:T(2,128)S(1)} %reshape.300, f32[]{:T(128)} %constant.83.clone.1), window={size=1x1x1x128 pad=0_0x0_0x0_0x127_0}, to_apply=%region_6.7 | reduce-window | flops 520192 | bytes 32772 | tf_op jit(solution)/shard_map/reduce-window.2
  34.9 1.8 %slice_bitcast_fusion = (bf16[1024,128]{1,0:T(8,128)(2,1)}, bf16[1024,128]{1,0:T(8,128)(2,1)S(1)}) fusion(bf16[2,1024,128]{2,1,0:T(8,128)(2,1)} %param.18), kind=kLoop, calls=%fused_computation.70 | loop fusion | bytes 1048576 | tf_op jit(solution)/shard_map/squeeze | solution.py:99
  36.6 0.3 rev.16
  36.9 0.8 convert_element_type.78
  37.8 0.4 reshape.310
  38.2 0.5 copy.176
  38.7 0.6 exponential_bitcast_fusion
  39.3 2.0 %convolution_bitcast_fusion.2 = f32[4,4,64,128]{3,2,1,0:T(8,128)S(1)} fusion(bf16[4,256,4,64]{1,3,2,0:T(8,128)(2,1)S(1)} %copy.176, f32[4,4,256]{2,1,0:T(4,128)S(1)} %get-tuple-element.324, f32[4,256,128]{2,1,0:T(8,128)} %convert_element_type.78), kind=kOutput, calls=%fused_computation.47 | convolution fusion | flops 68157440 | bytes 1589248 | tf_op jit(solution)/shard_map/cshp,chsn->chpn/dot_general | solution.py:42
  41.4 0.6 while.45
  42.3 0.4 copy-done.2
  42.7 2.0 %all_gather.6 = bf16[2,2,4,8193]{3,2,1,0:T(4,128)(2,1)S(1)} all-gather(bf16[1,2,4,8193]{3,2,1,0:T(4,128)(2,1)S(1)} %maximum_maximum_fusion), channel_id=1, replica_groups=mesh['seq'=2,'chan'=16,'batch'=8] {'seq'}, dimensions={0}, use_global_device_ids=true | all-gather | bytes 393264 | tf_op jit(solution)/shard_map/all_gather | solution.py:13
  44.7 0.2 slice_convert_fusion
  44.9 0.4 reshape.307
  45.4 3.2 %rev.18 = bf16[1024,128]{1,0:T(8,128)(2,1)S(1)} reverse(bf16[1024,128]{1,0:T(8,128)(2,1)} %get-tuple-element.319), dimensions={0} | reverse | bytes 524288 | tf_op jit(solution)/shard_map/rev | solution.py:99
  48.7 0.6 subtract_exponential_fusion
  49.3 0.3 fusion.58
  49.6 3.1 %fusion.22 = f32[4,256,4,64]{1,3,2,0:T(8,128)} fusion(bf16[4,256,4,64]{1,3,2,0:T(8,128)(2,1)S(1)} %copy.176, f32[4,4,256]{2,1,0:T(4,128)} %bitcast.166, f32[4,4,256]{2,1,0:T(4,128)S(1)} %copy-done.9, f32[4,256,256]{2,1,0:T(8,128)S(1)} %fusion.58, pred[256,256]{1,0:T(8,128)(4,1)S(1)} %iota_compare_fusion), kind=kOutput, calls=%fused_computation.37 | convolution fusion | flops 140509184 | bytes 2719744 | tf_op jit(solution)/shard_map/chts,cshp->cthp/dot_general | solution.py:38
  52.7 0.3 while.46
  53.0 0.7 copy-done.3
  53.8 1.6 fusion.25
  55.4 0.7 copy.180
  56.3 1.5 rev.19
  57.8 0.3 fusion.57
  58.2 2.5 %fusion.23 = f32[4,256,4,64]{1,3,2,0:T(8,128)S(1)} fusion(f32[4,4,256]{2,1,0:T(4,128)S(1)} %copy-done.13, f32[4,4,256]{2,1,0:T(4,128)S(1)} %copy-done.7, f32[4,256,256]{2,1,0:T(8,128)S(1)} %fusion.57, pred[256,256]{1,0:T(8,128)(4,1)S(1)} %copy-done.11, bf16[4,256,4,64]{1,0,3,2:T(4,128)(2,1)} %reshape.298), kind=kOutput, calls=%fused_computation.38 | convolution fusion | flops 140509184 | bytes 2719744 | tf_op jit(solution)/shard_map/chts,cshp->cthp/dot_general | solution.py:38
  60.7 0.3 fusion.27
  61.1 0.7 copy.178
  61.8 1.2 copy.198
  62.9 0.2 copy.182
  63.3 1.8 %multiply_reduce_fusion = (f32[1024]{0:T(1024)S(1)}, f32[1024,256]{0,1:T(8,128)S(1)}) fusion(bf16[1024,256]{0,1:T(8,128)(2,1)S(1)} %copy.182, f32[256]{0:T(256)S(1)} %mul.274, bf16[1024,256]{0,1:T(8,128)(2,1)S(1)} %copy.167, f32[1024,256]{0,1:T(8,128)} %bitcast.150, f32[1024,256]{0,1:T(8,128)S(1)} %rev.19), kind=kLoop, calls=%fused_computation.55 | loop fusion | flops 3144704 | bytes 4199424 | tf_op jit(solution)/shard_map/reduce_sum | solution.py:143
  65.2 15.2 %all_to_all.46 = f32[16,1,1024]{2,1,0:T(1,128)S(1)} all-to-all(f32[16,1,1024]{2,1,0:T(1,128)S(1)} %broadcast_in_dim.57), channel_id=1, replica_groups=mesh['seq'=2,'chan'=16,'batch'=8] {'chan'}, dimensions={0} | all-to-all | bytes 131072 | tf_op jit(solution)/shard_map/all_to_all | solution.py:23
  80.8 18.8 %all_to_all.44 = bf16[16,64,256]{2,1,0:T(8,128)(2,1)S(1)} all-to-all(bf16[16,64,256]{2,1,0:T(8,128)(2,1)S(1)} %bitcast.160), channel_id=1, replica_groups=mesh['seq'=2,'chan'=16,'batch'=8] {'chan'}, dimensions={0} | all-to-all | bytes 1048576 | tf_op jit(solution)/shard_map/all_to_all | solution.py:146
  99.7 42.4 %all-gather.2.cloned.1.call-done = bf16[4096,2048]{1,0:T(8,128)(2,1)} async-done(((bf16[4096,128]{1,0:T(8,128)(2,1)}), bf16[4096,2048]{1,0:T(8,128)(2,1)}) %all-gather.2.cloned.1.call-update) | async-done | bytes 16777232 | tf_op jit(solution)/shard_map/all_gather | solution.py:149
  142.1 8.8 %fusion.28 = bf16[8,16,8,128]{3,2,1,0:T(8,128)(2,1)S(1)} fusion(bf16[64,4096]{1,0:T(8,128)(2,1)S(1)} %bitcast.151, bf16[4096,2048]{1,0:T(8,128)(2,1)} %all-gather.2.cloned.1.call-done), kind=kOutput, calls=%fused_computation.49 | convolution fusion | flops 1073872896 | bytes 17563648 | tf_op jit(solution)/shard_map/dot_general | solution.py:147
  150.9 12.9 %all_to_all.45 = bf16[64,16,128]{2,0,1:T(8,128)(2,1)S(1)} all-to-all(bf16[64,16,128]{2,0,1:T(8,128)(2,1)S(1)} %bitcast.162), channel_id=1, replica_groups=mesh['seq'=2,'chan'=16,'batch'=8] {'chan'}, dimensions={1} | all-to-all | bytes 524288 | tf_op jit(solution)/shard_map/all_to_all | solution.py:152
  163.8 0.7 copy.241
  (119 shorter events, 4.4 us)
Async XLA Ops:
  6.5 135.5 %all-gather.2.cloned.1.call-start = ((), (), s32[]{:S(2)}) async-start(), calls=%async_computation.3 | async-start | bytes 17825792 | tf_op jit(solution)/shard_map/all_gather | solution.py:149
  17.9 20.8 %copy-start.5 = (f32[4,1024]{1,0:T(4,128)}, f32[4,1024]{1,0:T(4,128)S(1)}, u32[]{:S(2)}) copy-start(f32[4,1024]{1,0:T(4,128)S(1)} %rev.15) | copy-start | bytes 49156
  18.0 10.6 %copy-start.12 = (f32[4,4,256]{2,1,0:T(4,128)}, f32[4,4,256]{2,1,0:T(4,128)S(1)}, u32[]{:S(2)}) copy-start(f32[4,4,256]{2,1,0:T(4,128)S(1)} %get-tuple-element.314) | copy-start | bytes 49156
  23.3 3.3 %copy-start.6 = (f32[4,4,256]{2,1,0:T(4,128)}, f32[4,4,256]{2,1,0:T(4,128)S(1)}, u32[]{:S(2)}) copy-start(f32[4,4,256]{2,1,0:T(4,128)S(1)} %reduce_window_sum.59) | copy-start | bytes 49156
  29.2 7.5 %copy-start = (f32[4,4,64,128]{3,2,1,0:T(8,128)}, f32[4,4,64,128]{3,2,1,0:T(8,128)S(1)}, u32[]{:S(2)}) copy-start(f32[4,4,64,128]{3,2,1,0:T(8,128)S(1)} %get-tuple-element.216) | copy-start | bytes 1572868
  29.2 7.7 %copy-start.16 = (f32[4,4]{1,0:T(4,128)}, f32[4,4]{1,0:T(4,128)S(1)}, u32[]{:S(2)}) copy-start(f32[4,4]{1,0:T(4,128)S(1)} %get-tuple-element.516) | copy-start | bytes 196
  34.6 6.8 %copy-start.8 = (f32[4,4,256]{2,1,0:T(4,128)}, f32[4,4,256]{2,1,0:T(4,128)S(1)}, u32[]{:S(2)}) copy-start(f32[4,4,256]{2,1,0:T(4,128)S(1)} %reduce_window_sum.62) | copy-start | bytes 49156
  42.0 0.8 copy-start.2
  42.0 7.6 %copy-start.9 = (f32[4,4,256]{2,1,0:T(4,128)S(1)}, f32[4,4,256]{2,1,0:T(4,128)}, u32[]{:S(2)}) copy-start(f32[4,4,256]{2,1,0:T(4,128)} %copy-done.8) | copy-start | bytes 49156
  48.7 4.1 %copy-start.10 = (pred[256,256]{1,0:T(8,128)(4,1)}, pred[256,256]{1,0:T(8,128)(4,1)S(1)}, u32[]{:S(2)}) copy-start(pred[256,256]{1,0:T(8,128)(4,1)S(1)} %iota_compare_fusion) | copy-start | bytes 196612
  52.7 1.0 copy-start.3
  52.7 1.0 copy-start.15
  55.3 2.4 %copy-start.17 = (f32[4,4]{1,0:T(4,128)S(1)}, f32[4,4]{1,0:T(4,128)}, u32[]{:S(2)}) copy-start(f32[4,4]{1,0:T(4,128)} %copy-done.16) | copy-start | bytes 196
  55.3 2.8 %copy-start.7 = (f32[4,4,256]{2,1,0:T(4,128)S(1)}, f32[4,4,256]{2,1,0:T(4,128)}, u32[]{:S(2)}) copy-start(f32[4,4,256]{2,1,0:T(4,128)} %copy-done.6) | copy-start | bytes 49156
  55.4 2.8 %copy-start.11 = (pred[256,256]{1,0:T(8,128)(4,1)S(1)}, pred[256,256]{1,0:T(8,128)(4,1)}, u32[]{:S(2)}) copy-start(pred[256,256]{1,0:T(8,128)(4,1)} %copy-done.10) | copy-start | bytes 196612
  55.4 2.8 %copy-start.13 = (f32[4,4,256]{2,1,0:T(4,128)S(1)}, f32[4,4,256]{2,1,0:T(4,128)}, u32[]{:S(2)}) copy-start(f32[4,4,256]{2,1,0:T(4,128)} %copy-done.12) | copy-start | bytes 49156
  58.2 2.5 %copy-start.1 = (f32[4,4,64,128]{3,2,1,0:T(8,128)S(1)}, f32[4,4,64,128]{3,2,1,0:T(8,128)}, u32[]{:S(2)}) copy-start(f32[4,4,64,128]{3,2,1,0:T(8,128)} %copy-done) | copy-start | bytes 1572868
  58.2 2.5 %copy-start.14 = (f32[4,256,4]{1,2,0:T(4,128)S(1)}, f32[4,256,4]{1,2,0:T(4,128)}, u32[]{:S(2)}) copy-start(f32[4,256,4]{1,2,0:T(4,128)} %get-tuple-element.330) | copy-start | bytes 49156
  60.7 2.3 %copy-start.4 = (bf16[1024,256]{1,0:T(8,128)(2,1)S(1)}, bf16[1024,256]{1,0:T(8,128)(2,1)}, u32[]{:S(2)}) copy-start(bf16[1024,256]{1,0:T(8,128)(2,1)} %param.16) | copy-start | bytes 1572868
  60.7 2.5 %copy-start.19 = (f32[4]{0:T(128)S(1)}, f32[4]{0:T(128)}, u32[]{:S(2)}) copy-start(f32[4]{0:T(128)} %param.21) | copy-start | bytes 52
  61.8 18.7 %copy-start.18 = (f32[256]{0:T(256)S(1)}, f32[256]{0:T(256)}, u32[]{:S(2)}) copy-start(f32[256]{0:T(256)} %param.22) | copy-start | bytes 3076
Sparse Core Ops, SparseCore 0:
  9.7 132.2 all-gather.1
where the time goes:
time: 173 us; the launch traced here: 171 us
  blocking collectives  48.9 us (28%)
  waiting for transfers between devices  43.1 us (25%)
  local copies, waits for them, and re-layouts  26 us (15%)
  matrix products  20.8 us (12%)
  other arithmetic  18.2 us (11%)
  between operations  14 us (8%)
    all_gather x1, waiting for transfers between devices, body(): lax.all_gather(out_weight, 'chan', axis=1, tiled=True)  42.4 us
    all_to_all x1, blocking collectives, body(): lax.all_to_all(normed, 'chan', split_axis=0, concat_axis=1, tiled=True)  18.8 us
    all_to_all x1, blocking collectives, copy_for_each(): return lax.all_to_all(copies, axis, split_axis=0, concat_axis=0, tiled=True)  15.2 us
    all_to_all x1, blocking collectives, body(): lax.all_to_all(projected, 'chan', split_axis=1, concat_axis=0, tiled=True)  12.9 us
    another operation x8, other arithmetic  9.88 us
    dot_general x1, matrix products, body(): jnp.dot(frame_share, lax.all_gather(out_weight, 'chan', axis=1, tiled=Tru...  8.79 us
    rev x1, local copies, waits for them, and re-layouts, body(): ssm_input[::-1].reshape(shape_x)  6.33 us
    dot_general x2, matrix products, local_scan(): jnp.einsum('chts,cshp->cthp', weights, blocks_x, preferred_element_type=j...  5.62 us
  transfers between devices with their start and end apart: 1, of which 1 were waited for; matrix products, arithmetic and copies ran while one was open for 32% of the time, Pallas kernels for 0%

commit v1 on v0

--- a/solution.py
+++ b/solution.py
@@ -5,6 +5,14 @@
 
 SPAN = 256
 INNER = 4096
+
+
+def _resolve_leaf(mine):
+    d_next = jnp.concatenate(
+        lax.all_to_all(jnp.stack(jnp.split(mine, lax.axis_size("chan"), axis=1)), "chan", 0, 0),
+        axis=0,
+    )
+    return d_next
 
 
 def sent_together(arrays, axis, dim, along):
@@ -149,7 +157,7 @@
         lax.all_gather(out_weight, "chan", axis=1, tiled=True),
         preferred_element_type=jnp.float32,
     ).astype(jnp.bfloat16)
-    return lax.all_to_all(projected, "chan", split_axis=1, concat_axis=0, tiled=True)
+    return _resolve_leaf(projected)
 
 
 def solution(mesh):

time: 173 us -> 174 us (level)
    all_to_all x1, blocking collectives: 18.8 us -> 17 us  [body(): lax.all_to_all(normed, 'chan', split_axis=0, concat_axis=1, tiled=True)]
    unnamed x47 -> x54, local copies, waits for them, and re-layouts: 4.97 us -> 5.2 us
  transfers between devices with their start and end apart: 1 -> 1, of which waited for: 1 -> 1; matrix products, arithmetic and copies ran while one was open for 32% -> 31% of each run, Pallas kernels for 0% -> 0%
where the time goes in v1:
time: 174 us; the launch traced here: 171 us
  blocking collectives  47.4 us (27%)
  waiting for transfers between devices  44.5 us (26%)
  local copies, waits for them, and re-layouts  26.2 us (15%)
  matrix products  20.8 us (12%)
  other arithmetic  17.6 us (10%)
  between operations  14 us (8%)
    all_gather x1, waiting for transfers between devices, body(): lax.all_gather(out_weight, 'chan', axis=1, tiled=True)  43.8 us
    all_to_all x1, blocking collectives, body(): lax.all_to_all(normed, 'chan', split_axis=0, concat_axis=1, tiled=True)  17 us
    all_to_all x1, blocking collectives, copy_for_each(): return lax.all_to_all(copies, axis, split_axis=0, concat_axis=0, tiled=True)  15.2 us
    all_to_all x1, blocking collectives, _resolve_leaf(): lax.all_to_all(jnp.stack(jnp.split(mine, lax.axis_size('chan'), axis=1)),...  13.3 us
    another operation x8, other arithmetic  9.88 us
    dot_general x1, matrix products, body(): jnp.dot(frame_share, lax.all_gather(out_weight, 'chan', axis=1, tiled=Tru...  8.79 us
    rev x1, local copies, waits for them, and re-layouts, body(): ssm_input[::-1].reshape(shape_x)  6.33 us
    dot_general x2, matrix products, local_scan(): jnp.einsum('chts,cshp->cthp', weights, blocks_x, preferred_element_type=j...  5.64 us
  transfers between devices with their start and end apart: 1, of which 1 were waited for; matrix products, arithmetic and copies ran while one was open for 31% of the time, Pallas kernels for 0%

profile of v1, /device:TPU:96, one launch (start us, length us, event | category | flops | bytes accessed | tf_op | source)
XLA Modules:
  0.0 171.0 jit_solution(10512512988679347163)
XLA Ops:
  6.5 0.7 all-gather.2.cloned.1.call-update
  7.3 1.2 copy.160
  8.5 6.3 %rev.17 = bf16[1024,256]{1,0:T(8,128)(2,1)S(1)} reverse(bf16[1024,256]{1,0:T(8,128)(2,1)} %param.15), dimensions={0} | reverse | bytes 1048576 | tf_op jit(solution)/shard_map/rev | solution.py:105
  14.9 0.7 slice.57
  15.6 0.8 negate_bitcast_fusion
  16.4 0.8 compare_select_fusion
  17.2 0.7 rev.15
  18.0 4.8 %reduce-window.14 = f32[4,4,2,128]{3,2,1,0:T(2,128)S(1)} reduce-window(f32[4,4,2,128]{3,2,1,0:T(2,128)S(1)} %reshape.296, f32[]{:T(128)} %constant.83.clone.1), window={size=1x1x1x128 pad=0_0x0_0x0_0x127_0}, to_apply=%region_0.1 | reduce-window | flops 520192 | bytes 32772 | tf_op jit(solution)/shard_map/reduce-window
  23.6 1.1 fusion.55
  24.8 1.2 reshape.298
  26.0 0.6 exponential_multiply_fusion.1
  26.6 1.9 %convolution_bitcast_fusion.3 = f32[4,4,64,128]{3,2,1,0:T(8,128)S(1)} fusion(f32[4,4,256]{2,1,0:T(4,128)S(1)} %get-tuple-element.329, f32[4,256,128]{2,1,0:T(8,128)S(1)} %convert_element_type.76, bf16[4,256,4,64]{1,0,3,2:T(4,128)(2,1)} %reshape.298), kind=kOutput, calls=%fused_computation.48 | convolution fusion | flops 68157440 | bytes 1589248 | tf_op jit(solution)/shard_map/cshp,chsn->chpn/dot_general | solution.py:50
  28.6 0.6 while.44
  29.2 4.8 %reduce-window.16 = f32[4,4,2,128]{3,2,1,0:T(2,128)S(1)} reduce-window(f32[4,4,2,128]{3,2,1,0:T(2,128)S(1)} %reshape.300, f32[]{:T(128)} %constant.83.clone.1), window={size=1x1x1x128 pad=0_0x0_0x0_0x127_0}, to_apply=%region_6.7 | reduce-window | flops 520192 | bytes 32772 | tf_op jit(solution)/shard_map/reduce-window.2
  34.8 1.8 %slice_bitcast_fusion = (bf16[1024,128]{1,0:T(8,128)(2,1)}, bf16[1024,128]{1,0:T(8,128)(2,1)S(1)}) fusion(bf16[2,1024,128]{2,1,0:T(8,128)(2,1)} %param.18), kind=kLoop, calls=%fused_computation.68 | loop fusion | bytes 1048576 | tf_op jit(solution)/shard_map/squeeze | solution.py:107
  36.6 0.3 rev.16
  36.9 0.8 convert_element_type.78
  37.7 0.4 reshape.311
  38.1 0.5 copy.169
  38.7 0.6 exponential_bitcast_fusion
  39.3 2.0 %convolution_bitcast_fusion.2 = f32[4,4,64,128]{3,2,1,0:T(8,128)S(1)} fusion(bf16[4,256,4,64]{1,3,2,0:T(8,128)(2,1)S(1)} %copy.169, f32[4,4,256]{2,1,0:T(4,128)S(1)} %get-tuple-element.324, f32[4,256,128]{2,1,0:T(8,128)} %convert_element_type.78), kind=kOutput, calls=%fused_computation.47 | convolution fusion | flops 68157440 | bytes 1589248 | tf_op jit(solution)/shard_map/cshp,chsn->chpn/dot_general | solution.py:50
  41.3 0.6 while.45
  42.3 0.4 copy-done.2
  42.7 2.0 %all_gather.6 = bf16[2,2,4,8193]{3,2,1,0:T(4,128)(2,1)S(1)} all-gather(bf16[1,2,4,8193]{3,2,1,0:T(4,128)(2,1)S(1)} %maximum_maximum_fusion), channel_id=1, replica_groups=mesh['seq'=2,'chan'=16,'batch'=8] {'seq'}, dimensions={0}, use_global_device_ids=true | all-gather | bytes 393264 | tf_op jit(solution)/shard_map/all_gather | solution.py:21
  44.7 0.2 slice_convert_fusion
  44.9 0.4 reshape.308
  45.3 3.2 %rev.18 = bf16[1024,128]{1,0:T(8,128)(2,1)S(1)} reverse(bf16[1024,128]{1,0:T(8,128)(2,1)} %get-tuple-element.319), dimensions={0} | reverse | bytes 524288 | tf_op jit(solution)/shard_map/rev | solution.py:107
  48.6 0.3 fusion.57
  48.9 3.1 %fusion.22 = f32[4,256,4,64]{1,3,2,0:T(8,128)} fusion(bf16[4,256,4,64]{1,3,2,0:T(8,128)(2,1)S(1)} %copy.169, f32[4,4,256]{2,1,0:T(4,128)} %bitcast.222, f32[4,4,256]{2,1,0:T(4,128)S(1)} %copy-done.9, f32[4,256,256]{2,1,0:T(8,128)S(1)} %fusion.57, pred[256,256]{1,0:T(8,128)(4,1)S(1)} %iota_compare_fusion), kind=kOutput, calls=%fused_computation.37 | convolution fusion | flops 140509184 | bytes 2719744 | tf_op jit(solution)/shard_map/chts,cshp->cthp/dot_general | solution.py:46
  52.1 0.3 while.46
  52.4 0.7 copy-done.3
  53.1 1.6 fusion.25
  54.7 0.7 copy.173
  55.6 1.5 rev.19
  57.2 0.3 fusion.56
  57.5 2.5 %fusion.23 = f32[4,256,4,64]{1,3,2,0:T(8,128)S(1)} fusion(f32[4,4,256]{2,1,0:T(4,128)S(1)} %copy-done.11, f32[4,4,256]{2,1,0:T(4,128)S(1)} %copy-done.7, f32[4,256,256]{2,1,0:T(8,128)S(1)} %fusion.56, pred[256,256]{1,0:T(8,128)(4,1)S(1)} %iota_compare_fusion, bf16[4,256,4,64]{1,0,3,2:T(4,128)(2,1)} %reshape.298), kind=kOutput, calls=%fused_computation.38 | convolution fusion | flops 140509184 | bytes 2719744 | tf_op jit(solution)/shard_map/chts,cshp->cthp/dot_general | solution.py:46
  60.1 0.4 fusion.27
  60.4 0.7 copy.171
  61.1 1.2 copy.189
  62.3 0.2 copy.175
  62.7 1.8 %multiply_reduce_fusion = (f32[1024]{0:T(1024)S(1)}, f32[1024,256]{0,1:T(8,128)S(1)}) fusion(bf16[1024,256]{0,1:T(8,128)(2,1)S(1)} %copy.175, f32[256]{0:T(256)S(1)} %mul.274, bf16[1024,256]{0,1:T(8,128)(2,1)S(1)} %copy.160, f32[1024,256]{0,1:T(8,128)} %bitcast.207, f32[1024,256]{0,1:T(8,128)S(1)} %rev.19), kind=kLoop, calls=%fused_computation.54 | loop fusion | flops 3144704 | bytes 4199424 | tf_op jit(solution)/shard_map/reduce_sum | solution.py:151
  64.6 15.2 %all_to_all.32 = f32[16,1,1024]{2,1,0:T(1,128)S(1)} all-to-all(f32[16,1,1024]{2,1,0:T(1,128)S(1)} %broadcast_in_dim.57), channel_id=1, replica_groups=mesh['seq'=2,'chan'=16,'batch'=8] {'chan'}, dimensions={0} | all-to-all | bytes 131072 | tf_op jit(solution)/shard_map/all_to_all | solution.py:31
  80.0 0.2 copy.177
  80.2 17.0 %all_to_all.30 = bf16[16,64,256]{2,1,0:T(8,128)(2,1)S(1)} all-to-all(bf16[16,64,256]{2,1,0:T(8,128)(2,1)S(1)} %bitcast.217), channel_id=1, replica_groups=mesh['seq'=2,'chan'=16,'batch'=8] {'chan'}, dimensions={0} | all-to-all | bytes 1048576 | tf_op jit(solution)/shard_map/all_to_all | solution.py:154
  97.2 43.8 %all-gather.2.cloned.1.call-done = bf16[4096,2048]{1,0:T(8,128)(2,1)} async-done(((bf16[4096,128]{1,0:T(8,128)(2,1)}), bf16[4096,2048]{1,0:T(8,128)(2,1)}) %all-gather.2.cloned.1.call-update) | async-done | bytes 16777232 | tf_op jit(solution)/shard_map/all_gather | solution.py:157
  141.0 8.8 %convolution_convert_fusion = bf16[64,2048]{1,0:T(8,128)(2,1)S(1)} fusion(bf16[64,4096]{1,0:T(8,128)(2,1)S(1)} %bitcast.208, bf16[4096,2048]{1,0:T(8,128)(2,1)} %all-gather.2.cloned.1.call-done), kind=kOutput, calls=%fused_computation.20 | convolution fusion | flops 1073872896 | bytes 17563648 | tf_op jit(solution)/shard_map/dot_general | solution.py:155
  150.1 13.3 %all_to_all.31 = bf16[16,64,128]{2,1,0:T(8,128)(2,1)S(1)} all-to-all(bf16[16,64,128]{2,1,0:T(8,128)(2,1)S(1)} %constant_dynamic-update-slice_fusion), channel_id=1, replica_groups=mesh['seq'=2,'chan'=16,'batch'=8] {'chan'}, dimensions={0} | all-to-all | bytes 524288 | tf_op jit(solution)/shard_map/all_to_all | solution.py:12
  163.4 0.7 copy.245
  (126 shorter events, 4.3 us)
Async XLA Ops:
  6.5 134.5 %all-gather.2.cloned.1.call-start = ((), (), s32[]{:S(2)}) async-start(), calls=%async_computation.3 | async-start | bytes 17825792 | tf_op jit(solution)/shard_map/all_gather | solution.py:157
  17.9 20.8 %copy-start.5 = (f32[4,1024]{1,0:T(4,128)}, f32[4,1024]{1,0:T(4,128)S(1)}, u32[]{:S(2)}) copy-start(f32[4,1024]{1,0:T(4,128)S(1)} %rev.15) | copy-start | bytes 49156
  18.0 10.6 %copy-start.10 = (f32[4,4,256]{2,1,0:T(4,128)}, f32[4,4,256]{2,1,0:T(4,128)S(1)}, u32[]{:S(2)}) copy-start(f32[4,4,256]{2,1,0:T(4,128)S(1)} %get-tuple-element.314) | copy-start | bytes 49156
  23.3 3.3 %copy-start.6 = (f32[4,4,256]{2,1,0:T(4,128)}, f32[4,4,256]{2,1,0:T(4,128)S(1)}, u32[]{:S(2)}) copy-start(f32[4,4,256]{2,1,0:T(4,128)S(1)} %reduce_window_sum.59) | copy-start | bytes 49156
  29.2 7.5 %copy-start = (f32[4,4,64,128]{3,2,1,0:T(8,128)}, f32[4,4,64,128]{3,2,1,0:T(8,128)S(1)}, u32[]{:S(2)}) copy-start(f32[4,4,64,128]{3,2,1,0:T(8,128)S(1)} %get-tuple-element.216) | copy-start | bytes 1572868
  34.5 6.8 %copy-start.8 = (f32[4,4,256]{2,1,0:T(4,128)}, f32[4,4,256]{2,1,0:T(4,128)S(1)}, u32[]{:S(2)}) copy-start(f32[4,4,256]{2,1,0:T(4,128)S(1)} %reduce_window_sum.62) | copy-start | bytes 49156
  41.9 0.8 copy-start.2
  41.9 7.0 %copy-start.9 = (f32[4,4,256]{2,1,0:T(4,128)S(1)}, f32[4,4,256]{2,1,0:T(4,128)}, u32[]{:S(2)}) copy-start(f32[4,4,256]{2,1,0:T(4,128)} %copy-done.8) | copy-start | bytes 49156
  52.1 1.0 copy-start.3
  52.1 1.0 copy-start.13
  54.7 2.8 %copy-start.7 = (f32[4,4,256]{2,1,0:T(4,128)S(1)}, f32[4,4,256]{2,1,0:T(4,128)}, u32[]{:S(2)}) copy-start(f32[4,4,256]{2,1,0:T(4,128)} %copy-done.6) | copy-start | bytes 49156
  54.7 2.8 %copy-start.11 = (f32[4,4,256]{2,1,0:T(4,128)S(1)}, f32[4,4,256]{2,1,0:T(4,128)}, u32[]{:S(2)}) copy-start(f32[4,4,256]{2,1,0:T(4,128)} %copy-done.10) | copy-start | bytes 49156
  57.5 2.5 %copy-start.1 = (f32[4,4,64,128]{3,2,1,0:T(8,128)S(1)}, f32[4,4,64,128]{3,2,1,0:T(8,128)}, u32[]{:S(2)}) copy-start(f32[4,4,64,128]{3,2,1,0:T(8,128)} %copy-done) | copy-start | bytes 1572868
  57.5 2.5 %copy-start.12 = (f32[4,256,4]{1,2,0:T(4,128)S(1)}, f32[4,256,4]{1,2,0:T(4,128)}, u32[]{:S(2)}) copy-start(f32[4,256,4]{1,2,0:T(4,128)} %get-tuple-element.330) | copy-start | bytes 49156
  60.0 2.3 %copy-start.4 = (bf16[1024,256]{1,0:T(8,128)(2,1)S(1)}, bf16[1024,256]{1,0:T(8,128)(2,1)}, u32[]{:S(2)}) copy-start(bf16[1024,256]{1,0:T(8,128)(2,1)} %param.16) | copy-start | bytes 1572868
  60.0 2.5 %copy-start.15 = (f32[4]{0:T(128)S(1)}, f32[4]{0:T(128)}, u32[]{:S(2)}) copy-start(f32[4]{0:T(128)} %param.21) | copy-start | bytes 52
  61.1 18.7 %copy-start.14 = (f32[256]{0:T(256)S(1)}, f32[256]{0:T(256)}, u32[]{:S(2)}) copy-start(f32[256]{0:T(256)} %param.22) | copy-start | bytes 3076
Sparse Core Ops, SparseCore 0:
  9.7 131.2 all-gather.1
